TPU v7x, 512 devices: a whole 4x8x8 slice. The times are simulated.
512 devices in a mesh: section: 16 (over y, core), dp: 32 (over x, z).
Axes of the slice: x: 4, y: 8, z: 8, core: 2. Of those that a mesh axis runs over, the one named last changes fastest.
Arguments:
- patch_tokens: bfloat16 [4, 32, 196, 1280], P(None, 'dp'), may hold values from -24 to 24
- visible: int32 [4, 32, 98], P(None, 'dp'), may hold values from 0 to 195, as said below
- keep_mask: int32 [4, 32, 98], P(None, 'dp'), may hold values from 0 to 1, as said below
- lengths: int32 [4], replicated, may hold values from 49 to 98
- qkv_weight: bfloat16 [16, 1280, 1920], P('section', 'dp'), may hold values from -4 to 4
- out_weight: bfloat16 [16, 640, 1280], P('section', 'dp'), may hold values from -0.25 to 0.25
- norm_gain: bfloat16 [16, 1280], P('section'), may hold values from 0.099609375 to 1.8984375
- targets: bfloat16 [16, 4, 32, 98, 1280], P('section', None, 'dp'), may hold values from -12 to 12
Outputs:
- hidden_states: bfloat16 [16, 4, 32, 98, 1280], P('section', None, 'dp')
- token_loss: float32 [4, 32, 98], P(None, 'dp')
- loss: float32 [4], replicated
Inputs may be any that keep to these rules, and one draw needn't show every extreme that they name: `visible`: the 98 entries of one image are different patch numbers. `keep_mask`: slot 0 of every image is 1.
All inputs are finite; a program needn't handle non-finite values.
Results may differ from a plain program's by a relative error of at most 0.019.
Values may be sent and summed in bfloat16 or wider, within the bound.
A program may use at most 128 MiB of HBM per device.

v0:
```python
import jax
import jax.numpy as jnp
from jax import lax
from jax.sharding import PartitionSpec as P

HEADS = 8
HDIM = 80


def joined_along(tiles, dim):
    tiles = jnp.moveaxis(tiles, 0, dim)
    lengths = tiles.shape
    return tiles.reshape(*lengths[:dim], lengths[dim] * lengths[dim + 1], *lengths[dim + 2 :])


def gather_packed(arrays, axis, dims):
    flat = jnp.concatenate([a.reshape(-1) for a in arrays])
    lines, at, outs = (lax.all_gather(flat, axis), 0, [])
    for a, dim in zip(arrays, dims):
        tiles = lines[:, at : at + a.size].reshape(-1, *a.shape)
        outs.append(joined_along(tiles, dim))
        at += a.size
    return tuple(outs)


def passed_along(block, axis, distance):
    devices = range(lax.axis_size(axis))
    route = [(i - distance, i) for i in devices if i - distance in devices]
    return lax.ppermute(block, axis, route)


def copy_for_each(x, axis):
    length = lax.axis_size(axis)
    return lax.all_to_all(jnp.broadcast_to(x[None], (length, *x.shape)), axis, 0, 0, tiled=True)


def of_everyone(x, axis):
    return copy_for_each(x, axis).sum(axis=0)


def packed_total(arrays, axis):
    ends = [0]
    for a in arrays:
        ends.append(ends[-1] + a.size)
    running = of_everyone(jnp.concatenate([a.ravel() for a in arrays]), axis)
    return tuple((running[b:e].reshape(a.shape) for a, b, e in zip(arrays, ends, ends[1:])))


def norm_rows(values):
    row_mean = jnp.mean(values, -1, keepdims=True)
    centered = values - row_mean
    variance = jnp.mean(centered * centered, -1, keepdims=True)
    return centered * lax.rsqrt(variance + 1e-06)


def encoder_layer(tokens_now, live_rows, norm_scale, w_qkv, w_out):
    images, row_count, model_width = tokens_now.shape
    normed = (norm_rows(tokens_now.astype(jnp.float32)) * norm_scale).astype(jnp.bfloat16)
    projections = jnp.dot(
        normed.reshape(images * row_count, model_width), w_qkv, preferred_element_type=jnp.float32
    ).astype(jnp.bfloat16)
    projections = projections.reshape(images, row_count, 3, HEADS, HDIM)
    queries = projections[:, :, 0]
    key_rows = projections[:, :, 1]
    value_rows = projections[:, :, 2]
    scores = jnp.einsum(
        "iqhe,ikhe->ihqk", queries, key_rows, preferred_element_type=jnp.float32
    ) * HDIM ** (-0.5)
    scores = jnp.where(live_rows[:, None, None, :], scores, -1e30)
    row_max = jnp.max(scores, -1, keepdims=True)
    weights = jnp.exp(scores - row_max)
    probabilities = (weights / jnp.sum(weights, -1, keepdims=True)).astype(jnp.bfloat16)
    context = jnp.einsum(
        "ihqk,ikhe->iqhe", probabilities, value_rows, preferred_element_type=jnp.float32
    ).astype(jnp.bfloat16)
    projected = jnp.dot(
        context.reshape(images * row_count, HEADS * HDIM), w_out, preferred_element_type=jnp.float32
    )
    return (
        tokens_now.astype(jnp.float32) + projected.reshape(images, row_count, model_width)
    ).astype(jnp.bfloat16)


def per_device(
    patch_tokens, visible, keep_mask, lengths, qkv_weight, out_weight, norm_gain, targets
):
    sections = lax.axis_size("section")
    section_index = lax.axis_index("section")
    micro_count, images, row_count = visible.shape
    model_width = patch_tokens.shape[3]
    w_qkv, w_out = gather_packed((qkv_weight[0], out_weight[0]), "dp", (0, 0))
    norm_scale = norm_gain[0].astype(jnp.float32)
    positions = jnp.arange(row_count, dtype=jnp.int32)
    live_all = (positions[None, None, :] < lengths[:, None, None]) & (keep_mask == 1)
    inject_order = jnp.argsort(-lengths, stable=True)

    def layer_with_error(tokens_now, live_rows, target_rows):
        layer_output = encoder_layer(tokens_now, live_rows, norm_scale, w_qkv, w_out)
        deviation = norm_rows(layer_output.astype(jnp.float32)) - target_rows.astype(jnp.float32)
        token_error = jnp.where(live_rows, jnp.mean(deviation * deviation, -1), jnp.float32(0.0))
        return (layer_output, token_error)

    def apply_layer(tokens_now, live_rows, target_rows):
        return layer_with_error(tokens_now, live_rows, target_rows)

    def pass_full(values):
        return passed_along(values, "section", 1)

    def advance(step_index, state_carry):
        received, hidden, token_part = state_carry
        slot_index = step_index - section_index
        active = (slot_index >= 0) & (slot_index < micro_count)
        batch_index = inject_order[jnp.clip(slot_index, 0, micro_count - 1)]
        fresh_index = inject_order[jnp.clip(step_index, 0, micro_count - 1)]
        fresh_tokens = jnp.take_along_axis(
            patch_tokens[fresh_index], visible[fresh_index][:, :, None], axis=1
        )
        layer_input = jnp.where(section_index == 0, fresh_tokens, received)
        live_rows = live_all[batch_index]
        target_rows = targets[0, batch_index]

        def working():
            return apply_layer(layer_input, live_rows, target_rows)

        def resting():
            return (jnp.zeros_like(layer_input), jnp.zeros(live_rows.shape, jnp.float32))

        layer_output, token_error = lax.cond(active, working, resting)
        masked_output = jnp.where(live_rows[:, :, None], layer_output, jnp.zeros_like(layer_output))
        hidden = lax.dynamic_update_index_in_dim(
            hidden, jnp.where(active, masked_output, hidden[batch_index]), batch_index, 0
        )
        token_part = lax.dynamic_update_index_in_dim(
            token_part, token_part[batch_index] + token_error, batch_index, 0
        )
        received = pass_full(layer_output)
        return (received, hidden, token_part)

    start_carry = (
        jnp.zeros((images, row_count, model_width), jnp.bfloat16),
        jnp.zeros((micro_count, images, row_count, model_width), jnp.bfloat16),
        jnp.zeros((micro_count, images, row_count), jnp.float32),
    )
    received, hidden, token_part = lax.fori_loop(
        0, micro_count + sections - 1, advance, start_carry
    )
    token_loss = of_everyone(token_part, "section")
    count_part = jnp.sum(live_all.astype(jnp.float32), axis=(1, 2))
    loss_total, count = packed_total((jnp.sum(token_loss, axis=(1, 2)), count_part), "dp")
    loss = loss_total / count
    return (hidden[None], token_loss, loss)


def solution(mesh):
    placed = (
        P(None, "dp", None, None),
        P(None, "dp", None),
        P(None, "dp", None),
        P(),
        P("section", "dp", None),
        P("section", "dp", None),
        P("section", None),
        P("section", None, "dp", None, None),
    )
    return jax.shard_map(
        per_device,
        mesh=mesh,
        in_specs=placed,
        out_specs=(P("section", None, "dp", None, None), P(None, "dp", None), P()),
        check_vma=False,
    )
```

profile of v0, /device:TPU:1, one launch (start us, length us, event | category | flops | bytes accessed | tf_op | source)
XLA Modules:
  0.0 572.5 jit_solution(10945011157844049402)
XLA Ops:
  14.5 97.9 %all-gather.3.cloned.1.call-done = bf16[3276800]{0:T(1024)(128)(2,1)} async-done(((bf16[102400]{0:T(1024)(128)(2,1)}), bf16[3276800]{0:T(1024)(128)(2,1)}) %all-gather.3.cloned.1.call-update) | async-done | bytes 6553616 | tf_op jit(solution)/shard_map/all_gather | solution.py:18
  112.4 7.3 %reshape.375 = bf16[32,102400]{1,0:T(8,128)(2,1)} reshape(bf16[3276800]{0:T(1024)(128)(2,1)} %all-gather.3.cloned.1.call-done) | data formatting | bytes 13107200 | tf_op jit(solution)/shard_map/all_gather | solution.py:18
  121.2 4.9 slice.45
  126.1 6.2 %reshape_reshape.6 = bf16[1280,1920]{1,0:T(8,128)(2,1)} reshape(bf16[32,76800]{1,0:T(8,128)(2,1)} %slice.45) | data formatting | bytes 9830400 | tf_op jit(solution)/shard_map/reshape;reshape | solution.py:13
  136.0 329.4 %while.18 = (s32[]{:T(128)}, bf16[1,98,1280]{2,1,0:T(8,128)(2,1)S(1)}, bf16[4,1,98,1280]{3,2,1,0:T(8,128)(2,1)}, f32[4,1,98]{2,1,0:T(1,128)S(1)}, s32[]{:T(128)}...) while((s32[]{:T(128)}, ...), condition=%wide.region_11.12_spmd, body=%wide.region_1.11_spmd.sunk | while | flops 683966464 | bytes 16245705 | solution.py:144
  139.3 4.0 collective-permute-start
  146.2 8.8 %collective-permute-done = bf16[1,98,1280]{2,1,0:T(8,128)(2,1)S(1)} collective-permute-done((bf16[1,98,1280]{2,1,0:T(8,128)(2,1)}, bf16[1,98,1280]{2,1,0:T(8,128)(2,1)S(1)}, u32[]{:S(2)}, u32[]{:S(2)}) %collective-permute-start) | collective-permute-done | bytes 250912 | tf_op jit(solution)/shard_map/while/body/eval_jaxpr/ppermute | solution.py:29
  157.6 12.8 %conditional.2 = (bf16[1,98,1280]{2,1,0:T(8,128)(2,1)}, f32[1,98]{1,0:T(1,128)S(1)}) conditional(s32[]{:T(128)} %convert_element_type.145, () %tuple.87, (pred[]{:T(512)}, s32[4,1,98]{2,1,0:T(1,128)S(1)}, s32[]{:T(128)}, bf16[4,1,196,1280]{3,2,1,0:T(8,128)(2,1)}, bf16[1,98,1280]{2,1,0:T(8,128)(2,1)S(1)}, /*index=5*/f32[1280]{0:T(1024)S(1)}, ...), branch_computations={%region_2.2_spmd, %region_3.10_spmd} | conditional | flops 683715456 | bytes 13954041 | solution.py:128
  178.6 12.9 %conditional.2 = (bf16[1,98,1280]{2,1,0:T(8,128)(2,1)}, f32[1,98]{1,0:T(1,128)S(1)}) conditional(s32[]{:T(128)} %convert_element_type.145, () %tuple.87, (pred[]{:T(512)}, s32[4,1,98]{2,1,0:T(1,128)S(1)}, s32[]{:T(128)}, bf16[4,1,196,1280]{3,2,1,0:T(8,128)(2,1)}, bf16[1,98,1280]{2,1,0:T(8,128)(2,1)S(1)}, /*index=5*/f32[1280]{0:T(1024)S(1)}, ...), branch_computations={%region_2.2_spmd, %region_3.10_spmd} | conditional | flops 683715456 | bytes 13954041 | solution.py:128
  191.5 4.3 collective-permute-start
  202.0 12.9 %conditional.2 = (bf16[1,98,1280]{2,1,0:T(8,128)(2,1)}, f32[1,98]{1,0:T(1,128)S(1)}) conditional(s32[]{:T(128)} %convert_element_type.145, () %tuple.87, (pred[]{:T(512)}, s32[4,1,98]{2,1,0:T(1,128)S(1)}, s32[]{:T(128)}, bf16[4,1,196,1280]{3,2,1,0:T(8,128)(2,1)}, bf16[1,98,1280]{2,1,0:T(8,128)(2,1)S(1)}, /*index=5*/f32[1280]{0:T(1024)S(1)}, ...), branch_computations={%region_2.2_spmd, %region_3.10_spmd} | conditional | flops 683715456 | bytes 13954041 | solution.py:128
  214.8 4.3 collective-permute-start
  225.4 12.9 %conditional.2 = (bf16[1,98,1280]{2,1,0:T(8,128)(2,1)}, f32[1,98]{1,0:T(1,128)S(1)}) conditional(s32[]{:T(128)} %convert_element_type.145, () %tuple.87, (pred[]{:T(512)}, s32[4,1,98]{2,1,0:T(1,128)S(1)}, s32[]{:T(128)}, bf16[4,1,196,1280]{3,2,1,0:T(8,128)(2,1)}, bf16[1,98,1280]{2,1,0:T(8,128)(2,1)S(1)}, /*index=5*/f32[1280]{0:T(1024)S(1)}, ...), branch_computations={%region_2.2_spmd, %region_3.10_spmd} | conditional | flops 683715456 | bytes 13954041 | solution.py:128
  229.7 3.4 convolution_convert_fusion
  238.2 4.3 collective-permute-start
  249.5 16.4 %collective-permute-start = (bf16[1,98,1280]{2,1,0:T(8,128)(2,1)}, bf16[1,98,1280]{2,1,0:T(8,128)(2,1)S(1)}, u32[]{:S(2)}, u32[]{:S(2)}) collective-permute-start(bf16[1,98,1280]{2,1,0:T(8,128)(2,1)} %get-tuple-element.751), channel_id=1, source_target_pairs={{0,32},{32,64},{64,96},{96,128},{128,160},{160,192},{192,224},{224... | collective-permute-start | bytes 752648 | tf_op jit(solution)/shard_map/while/body/eval_jaxpr/ppermute | solution.py:29
  272.9 4.3 collective-permute-start
  284.2 8.9 %collective-permute-start = (bf16[1,98,1280]{2,1,0:T(8,128)(2,1)}, bf16[1,98,1280]{2,1,0:T(8,128)(2,1)S(1)}, u32[]{:S(2)}, u32[]{:S(2)}) collective-permute-start(bf16[1,98,1280]{2,1,0:T(8,128)(2,1)} %get-tuple-element.751), channel_id=1, source_target_pairs={{0,32},{32,64},{64,96},{96,128},{128,160},{160,192},{192,224},{224... | collective-permute-start | bytes 752648 | tf_op jit(solution)/shard_map/while/body/eval_jaxpr/ppermute | solution.py:29
  300.1 4.3 collective-permute-start
  311.4 14.0 %collective-permute-start = (bf16[1,98,1280]{2,1,0:T(8,128)(2,1)}, bf16[1,98,1280]{2,1,0:T(8,128)(2,1)S(1)}, u32[]{:S(2)}, u32[]{:S(2)}) collective-permute-start(bf16[1,98,1280]{2,1,0:T(8,128)(2,1)} %get-tuple-element.751), channel_id=1, source_target_pairs={{0,32},{32,64},{64,96},{96,128},{128,160},{160,192},{192,224},{224... | collective-permute-start | bytes 752648 | tf_op jit(solution)/shard_map/while/body/eval_jaxpr/ppermute | solution.py:29
  332.4 4.3 collective-permute-start
  343.7 8.9 %collective-permute-start = (bf16[1,98,1280]{2,1,0:T(8,128)(2,1)}, bf16[1,98,1280]{2,1,0:T(8,128)(2,1)S(1)}, u32[]{:S(2)}, u32[]{:S(2)}) collective-permute-start(bf16[1,98,1280]{2,1,0:T(8,128)(2,1)} %get-tuple-element.751), channel_id=1, source_target_pairs={{0,32},{32,64},{64,96},{96,128},{128,160},{160,192},{192,224},{224... | collective-permute-start | bytes 752648 | tf_op jit(solution)/shard_map/while/body/eval_jaxpr/ppermute | solution.py:29
  359.6 4.3 collective-permute-start
  370.9 14.0 %collective-permute-start = (bf16[1,98,1280]{2,1,0:T(8,128)(2,1)}, bf16[1,98,1280]{2,1,0:T(8,128)(2,1)S(1)}, u32[]{:S(2)}, u32[]{:S(2)}) collective-permute-start(bf16[1,98,1280]{2,1,0:T(8,128)(2,1)} %get-tuple-element.751), channel_id=1, source_target_pairs={{0,32},{32,64},{64,96},{96,128},{128,160},{160,192},{192,224},{224... | collective-permute-start | bytes 752648 | tf_op jit(solution)/shard_map/while/body/eval_jaxpr/ppermute | solution.py:29
  391.9 4.3 collective-permute-start
  403.2 9.0 %collective-permute-start = (bf16[1,98,1280]{2,1,0:T(8,128)(2,1)}, bf16[1,98,1280]{2,1,0:T(8,128)(2,1)S(1)}, u32[]{:S(2)}, u32[]{:S(2)}) collective-permute-start(bf16[1,98,1280]{2,1,0:T(8,128)(2,1)} %get-tuple-element.751), channel_id=1, source_target_pairs={{0,32},{32,64},{64,96},{96,128},{128,160},{160,192},{192,224},{224... | collective-permute-start | bytes 752648 | tf_op jit(solution)/shard_map/while/body/eval_jaxpr/ppermute | solution.py:29
  419.1 5.5 collective-permute-start
  431.6 17.6 %collective-permute-start = (bf16[1,98,1280]{2,1,0:T(8,128)(2,1)}, bf16[1,98,1280]{2,1,0:T(8,128)(2,1)S(1)}, u32[]{:S(2)}, u32[]{:S(2)}) collective-permute-start(bf16[1,98,1280]{2,1,0:T(8,128)(2,1)} %get-tuple-element.751), channel_id=1, source_target_pairs={{0,32},{32,64},{64,96},{96,128},{128,160},{160,192},{192,224},{224... | collective-permute-start | bytes 752648 | tf_op jit(solution)/shard_map/while/body/eval_jaxpr/ppermute | solution.py:29
  456.2 5.5 collective-permute-start
  465.4 84.5 %all_to_all.11 = f32[16,4,1,98]{3,2,1,0:T(1,128)S(1)} all-to-all(f32[16,4,1,98]{3,2,1,0:T(1,128)S(1)} %broadcast_in_dim.104), channel_id=1, replica_groups=mesh['section'=16,'dp'=32] {'section'}, dimensions={0} | all-to-all | bytes 50176 | tf_op jit(solution)/shard_map/all_to_all | solution.py:34
  551.2 5.2 all-to-all-start.1
  559.0 6.1 %all-to-all-done.1 = f32[32,1,8]{2,1,0:T(1,128)S(1)} async-done(((f32[32,1,8]{2,1,0:T(1,128)}), f32[32,1,8]{2,1,0:T(1,128)S(1)}, u32[]{:S(2)}, u32[]{:S(2)}) %all-to-all-start.1) | async-done | bytes 1056 | tf_op jit(solution)/shard_map/all_to_all | solution.py:34
  (293 shorter events, 161.5 us)
Async XLA Ops:
  7.2 3.7 copy-start.1
  7.2 4.8 copy-start
  7.2 105.2 %all-gather.3.cloned.1.call-start = ((), (), s32[]{:S(2)}) async-start(), calls=%async_computation.2 | async-start | bytes 6758400 | tf_op jit(solution)/shard_map/all_gather | solution.py:18
  11.9 2.3 copy-start.2
  11.9 2.3 copy-start.3
  11.9 2.3 copy-start.4
  132.3 3.6 copy-start.5
  139.3 15.7 %collective-permute-start = (bf16[1,98,1280]{2,1,0:T(8,128)(2,1)}, bf16[1,98,1280]{2,1,0:T(8,128)(2,1)S(1)}, u32[]{:S(2)}, u32[]{:S(2)}) collective-permute-start(bf16[1,98,1280]{2,1,0:T(8,128)(2,1)} %get-tuple-element.751), channel_id=1, source_target_pairs={{0,32},{32,64},{64,96},{96,128},{128,160},{160,192},{192,224},{224... | collective-permute-start | bytes 752648 | tf_op jit(solution)/shard_map/while/body/eval_jaxpr/ppermute | solution.py:29
  170.4 5.6 collective-permute-start
  191.5 7.9 %collective-permute-start = (bf16[1,98,1280]{2,1,0:T(8,128)(2,1)}, bf16[1,98,1280]{2,1,0:T(8,128)(2,1)S(1)}, u32[]{:S(2)}, u32[]{:S(2)}) collective-permute-start(bf16[1,98,1280]{2,1,0:T(8,128)(2,1)} %get-tuple-element.751), channel_id=1, source_target_pairs={{0,32},{32,64},{64,96},{96,128},{128,160},{160,192},{192,224},{224... | collective-permute-start | bytes 752648 | tf_op jit(solution)/shard_map/while/body/eval_jaxpr/ppermute | solution.py:29
  214.8 8.0 %collective-permute-start = (bf16[1,98,1280]{2,1,0:T(8,128)(2,1)}, bf16[1,98,1280]{2,1,0:T(8,128)(2,1)S(1)}, u32[]{:S(2)}, u32[]{:S(2)}) collective-permute-start(bf16[1,98,1280]{2,1,0:T(8,128)(2,1)} %get-tuple-element.751), channel_id=1, source_target_pairs={{0,32},{32,64},{64,96},{96,128},{128,160},{160,192},{192,224},{224... | collective-permute-start | bytes 752648 | tf_op jit(solution)/shard_map/while/body/eval_jaxpr/ppermute | solution.py:29
  238.2 7.9 %collective-permute-start = (bf16[1,98,1280]{2,1,0:T(8,128)(2,1)}, bf16[1,98,1280]{2,1,0:T(8,128)(2,1)S(1)}, u32[]{:S(2)}, u32[]{:S(2)}) collective-permute-start(bf16[1,98,1280]{2,1,0:T(8,128)(2,1)} %get-tuple-element.751), channel_id=1, source_target_pairs={{0,32},{32,64},{64,96},{96,128},{128,160},{160,192},{192,224},{224... | collective-permute-start | bytes 752648 | tf_op jit(solution)/shard_map/while/body/eval_jaxpr/ppermute | solution.py:29
  249.5 20.1 %collective-permute-start = (bf16[1,98,1280]{2,1,0:T(8,128)(2,1)}, bf16[1,98,1280]{2,1,0:T(8,128)(2,1)S(1)}, u32[]{:S(2)}, u32[]{:S(2)}) collective-permute-start(bf16[1,98,1280]{2,1,0:T(8,128)(2,1)} %get-tuple-element.751), channel_id=1, source_target_pairs={{0,32},{32,64},{64,96},{96,128},{128,160},{160,192},{192,224},{224... | collective-permute-start | bytes 752648 | tf_op jit(solution)/shard_map/while/body/eval_jaxpr/ppermute | solution.py:29
  272.9 7.9 %collective-permute-start = (bf16[1,98,1280]{2,1,0:T(8,128)(2,1)}, bf16[1,98,1280]{2,1,0:T(8,128)(2,1)S(1)}, u32[]{:S(2)}, u32[]{:S(2)}) collective-permute-start(bf16[1,98,1280]{2,1,0:T(8,128)(2,1)} %get-tuple-element.751), channel_id=1, source_target_pairs={{0,32},{32,64},{64,96},{96,128},{128,160},{160,192},{192,224},{224... | collective-permute-start | bytes 752648 | tf_op jit(solution)/shard_map/while/body/eval_jaxpr/ppermute | solution.py:29
  284.2 12.6 %collective-permute-start = (bf16[1,98,1280]{2,1,0:T(8,128)(2,1)}, bf16[1,98,1280]{2,1,0:T(8,128)(2,1)S(1)}, u32[]{:S(2)}, u32[]{:S(2)}) collective-permute-start(bf16[1,98,1280]{2,1,0:T(8,128)(2,1)} %get-tuple-element.751), channel_id=1, source_target_pairs={{0,32},{32,64},{64,96},{96,128},{128,160},{160,192},{192,224},{224... | collective-permute-start | bytes 752648 | tf_op jit(solution)/shard_map/while/body/eval_jaxpr/ppermute | solution.py:29
  300.1 7.9 %collective-permute-start = (bf16[1,98,1280]{2,1,0:T(8,128)(2,1)}, bf16[1,98,1280]{2,1,0:T(8,128)(2,1)S(1)}, u32[]{:S(2)}, u32[]{:S(2)}) collective-permute-start(bf16[1,98,1280]{2,1,0:T(8,128)(2,1)} %get-tuple-element.751), channel_id=1, source_target_pairs={{0,32},{32,64},{64,96},{96,128},{128,160},{160,192},{192,224},{224... | collective-permute-start | bytes 752648 | tf_op jit(solution)/shard_map/while/body/eval_jaxpr/ppermute | solution.py:29
  311.4 17.7 %collective-permute-start = (bf16[1,98,1280]{2,1,0:T(8,128)(2,1)}, bf16[1,98,1280]{2,1,0:T(8,128)(2,1)S(1)}, u32[]{:S(2)}, u32[]{:S(2)}) collective-permute-start(bf16[1,98,1280]{2,1,0:T(8,128)(2,1)} %get-tuple-element.751), channel_id=1, source_target_pairs={{0,32},{32,64},{64,96},{96,128},{128,160},{160,192},{192,224},{224... | collective-permute-start | bytes 752648 | tf_op jit(solution)/shard_map/while/body/eval_jaxpr/ppermute | solution.py:29
  332.4 7.9 %collective-permute-start = (bf16[1,98,1280]{2,1,0:T(8,128)(2,1)}, bf16[1,98,1280]{2,1,0:T(8,128)(2,1)S(1)}, u32[]{:S(2)}, u32[]{:S(2)}) collective-permute-start(bf16[1,98,1280]{2,1,0:T(8,128)(2,1)} %get-tuple-element.751), channel_id=1, source_target_pairs={{0,32},{32,64},{64,96},{96,128},{128,160},{160,192},{192,224},{224... | collective-permute-start | bytes 752648 | tf_op jit(solution)/shard_map/while/body/eval_jaxpr/ppermute | solution.py:29
  343.7 12.6 %collective-permute-start = (bf16[1,98,1280]{2,1,0:T(8,128)(2,1)}, bf16[1,98,1280]{2,1,0:T(8,128)(2,1)S(1)}, u32[]{:S(2)}, u32[]{:S(2)}) collective-permute-start(bf16[1,98,1280]{2,1,0:T(8,128)(2,1)} %get-tuple-element.751), channel_id=1, source_target_pairs={{0,32},{32,64},{64,96},{96,128},{128,160},{160,192},{192,224},{224... | collective-permute-start | bytes 752648 | tf_op jit(solution)/shard_map/while/body/eval_jaxpr/ppermute | solution.py:29
  359.6 7.9 %collective-permute-start = (bf16[1,98,1280]{2,1,0:T(8,128)(2,1)}, bf16[1,98,1280]{2,1,0:T(8,128)(2,1)S(1)}, u32[]{:S(2)}, u32[]{:S(2)}) collective-permute-start(bf16[1,98,1280]{2,1,0:T(8,128)(2,1)} %get-tuple-element.751), channel_id=1, source_target_pairs={{0,32},{32,64},{64,96},{96,128},{128,160},{160,192},{192,224},{224... | collective-permute-start | bytes 752648 | tf_op jit(solution)/shard_map/while/body/eval_jaxpr/ppermute | solution.py:29
  370.9 17.7 %collective-permute-start = (bf16[1,98,1280]{2,1,0:T(8,128)(2,1)}, bf16[1,98,1280]{2,1,0:T(8,128)(2,1)S(1)}, u32[]{:S(2)}, u32[]{:S(2)}) collective-permute-start(bf16[1,98,1280]{2,1,0:T(8,128)(2,1)} %get-tuple-element.751), channel_id=1, source_target_pairs={{0,32},{32,64},{64,96},{96,128},{128,160},{160,192},{192,224},{224... | collective-permute-start | bytes 752648 | tf_op jit(solution)/shard_map/while/body/eval_jaxpr/ppermute | solution.py:29
  391.9 7.9 %collective-permute-start = (bf16[1,98,1280]{2,1,0:T(8,128)(2,1)}, bf16[1,98,1280]{2,1,0:T(8,128)(2,1)S(1)}, u32[]{:S(2)}, u32[]{:S(2)}) collective-permute-start(bf16[1,98,1280]{2,1,0:T(8,128)(2,1)} %get-tuple-element.751), channel_id=1, source_target_pairs={{0,32},{32,64},{64,96},{96,128},{128,160},{160,192},{192,224},{224... | collective-permute-start | bytes 752648 | tf_op jit(solution)/shard_map/while/body/eval_jaxpr/ppermute | solution.py:29
  403.2 12.6 %collective-permute-start = (bf16[1,98,1280]{2,1,0:T(8,128)(2,1)}, bf16[1,98,1280]{2,1,0:T(8,128)(2,1)S(1)}, u32[]{:S(2)}, u32[]{:S(2)}) collective-permute-start(bf16[1,98,1280]{2,1,0:T(8,128)(2,1)} %get-tuple-element.751), channel_id=1, source_target_pairs={{0,32},{32,64},{64,96},{96,128},{128,160},{160,192},{192,224},{224... | collective-permute-start | bytes 752648 | tf_op jit(solution)/shard_map/while/body/eval_jaxpr/ppermute | solution.py:29
  419.1 9.1 %collective-permute-start = (bf16[1,98,1280]{2,1,0:T(8,128)(2,1)}, bf16[1,98,1280]{2,1,0:T(8,128)(2,1)S(1)}, u32[]{:S(2)}, u32[]{:S(2)}) collective-permute-start(bf16[1,98,1280]{2,1,0:T(8,128)(2,1)} %get-tuple-element.751), channel_id=1, source_target_pairs={{0,32},{32,64},{64,96},{96,128},{128,160},{160,192},{192,224},{224... | collective-permute-start | bytes 752648 | tf_op jit(solution)/shard_map/while/body/eval_jaxpr/ppermute | solution.py:29
  431.6 21.3 %collective-permute-start = (bf16[1,98,1280]{2,1,0:T(8,128)(2,1)}, bf16[1,98,1280]{2,1,0:T(8,128)(2,1)S(1)}, u32[]{:S(2)}, u32[]{:S(2)}) collective-permute-start(bf16[1,98,1280]{2,1,0:T(8,128)(2,1)} %get-tuple-element.751), channel_id=1, source_target_pairs={{0,32},{32,64},{64,96},{96,128},{128,160},{160,192},{192,224},{224... | collective-permute-start | bytes 752648 | tf_op jit(solution)/shard_map/while/body/eval_jaxpr/ppermute | solution.py:29
  456.2 9.1 %collective-permute-start = (bf16[1,98,1280]{2,1,0:T(8,128)(2,1)}, bf16[1,98,1280]{2,1,0:T(8,128)(2,1)S(1)}, u32[]{:S(2)}, u32[]{:S(2)}) collective-permute-start(bf16[1,98,1280]{2,1,0:T(8,128)(2,1)} %get-tuple-element.751), channel_id=1, source_target_pairs={{0,32},{32,64},{64,96},{96,128},{128,160},{160,192},{192,224},{224... | collective-permute-start | bytes 752648 | tf_op jit(solution)/shard_map/while/body/eval_jaxpr/ppermute | solution.py:29
  551.2 13.8 %all-to-all-start.1 = ((f32[32,1,8]{2,1,0:T(1,128)}), f32[32,1,8]{2,1,0:T(1,128)S(1)}, u32[]{:S(2)}, u32[]{:S(2)}) async-start(f32[32,1,8]{2,1,0:T(1,128)} %broadcast_in_dim.105), calls=%async_computation.1 | async-start | bytes 32768 | tf_op jit(solution)/shard_map/all_to_all | solution.py:34
Sparse Core Ops, SparseCore 0:
  11.7 100.6 all-gather.2
where the time goes:
time: 576 us; the launch traced here: 573 us
  starting transfers between devices  145 us (25%)
  waiting for transfers between devices  127 us (22%)
  blocking collectives  84.5 us (15%)
  local copies, waits for them, and re-layouts  81.9 us (14%)
  other arithmetic  51.2 us (9%)
  loops' own time  45.7 us (8%)
  matrix products  22.4 us (4%)
  between operations  14.1 us (2%)
    ppermute x19, starting transfers between devices, passed_along(): return lax.ppermute(block, axis, route)  140 us
    all_gather x1, waiting for transfers between devices, gather_packed(): lines, at, outs = (lax.all_gather(flat, axis), 0, [])  97.9 us
    all_to_all x1, blocking collectives, copy_for_each(): lax.all_to_all(jnp.broadcast_to(x[None], (length, *x.shape)), axis, 0, 0,...  84.5 us
    another operation x1, loops' own time, per_device(): lax.fori_loop(0, micro_count + sections - 1, advance, start_carry)  37.6 us
    dynamic_update_slice x19, other arithmetic, advance(): lax.dynamic_update_index_in_dim(hidden, jnp.where(active, masked_output,...  34.9 us
    ppermute x19, waiting for transfers between devices, passed_along(): return lax.ppermute(block, axis, route)  23.4 us
    dynamic_slice x19, local copies, waits for them, and re-layouts, advance(): hidden[batch_index]  18.6 us
    dot_general x4, matrix products, encoder_layer(): jnp.dot(normed.reshape(images * row_count, model_width), w_qkv, preferred...  13.5 us
  transfers between devices with their start and end apart: 21, of which 21 were waited for; matrix products, arithmetic and copies ran while one was open for 11% of the time, Pallas kernels for 0%

commit v1 on v0

v1 whole, which is shorter than its diff:
```python
import functools

import jax
import jax.numpy as jnp
from jax import lax
from jax.experimental import pallas as pl
from jax.experimental.pallas import tpu as pltpu
from jax.sharding import PartitionSpec as P

HDIM = 80
SPLIT = 48
X = 4


def normalised(values):
    row_mean = jnp.mean(values, -1, keepdims=True)
    centered = values - row_mean
    variance = jnp.mean(centered * centered, -1, keepdims=True)
    return centered * lax.rsqrt(variance + 1e-06)


def gather_plan(xs, zs):
    waiting = []

    def one_way(part, where):
        out = []
        if part == 0:
            first, second = (zs, xs)
        else:
            first, second = (xs, zs)
        flows = {1: first // 2, -1: first - 1 - first // 2}
        cross = {1: second // 2, -1: second - 1 - second // 2}
        return (flows, cross)

    times = {}
    links = {}
    heap = []
    cost = {0: 2.6, 1: 1.8}

    def link_of(key, way, ring):
        part, f, s = key
        if ring == 0:
            sign = way
        else:
            sign = way if f % 2 == 0 else -way
        dim = ("z", "x")[part] if ring == 0 else ("x", "z")[part]
        return (dim, sign)

    def push(key, way, ring, ready):
        heap.append((ready, len(heap), key, way, ring))

    def arrived(key, ready):
        part, f, s = key
        flows, cross = one_way(part, None)
        if s == 0:
            for way in (1, -1):
                if (f == 0 or (f > 0) == (way > 0)) and abs(f) < flows[way]:
                    push((part, f + way, 0), way, 0, ready)
            for way in (1, -1):
                push((part, f, way), way, 1, ready + 0.01)
        else:
            way = 1 if s > 0 else -1
            if abs(s) < cross[way]:
                push((part, f, s + way), way, 1, ready)

    arrived((0, 0, 0), 0.0)
    arrived((1, 0, 0), 0.0)
    while heap:
        heap.sort()
        ready, _, key, way, ring = heap.pop(0)
        link = link_of(key, way, ring)
        begin = max(ready, links.get(link, 0.0))
        links[link] = begin + cost[key[0]]
        times[key] = begin + cost[key[0]] + 1.6
        arrived(key, times[key] + 0.1)
    return sorted(times, key=lambda key: times[key])


def kernel(
    dims,
    lengths_ref,
    visible_ref,
    keep_ref,
    wq_ref,
    wo_ref,
    gain_ref,
    patch_hbm,
    target_hbm,
    hidden_hbm,
    token_ref,
    loss_ref,
    slabs,
    wqkv,
    wout,
    patch,
    target,
    xin,
    yout,
    hid,
    qkv,
    ctx,
    err_in,
    err_out,
    live_rows,
    tl,
    part_own,
    part_mid,
    slots_x,
    slots_z,
    load_sem,
    hid_sem,
    own_recv,
    send_first,
    send_second,
    x_send,
    x_recv,
    e_send,
    e_recv,
    t_send,
    t_recv,
    rx_send,
    rx_recv,
    rz_send,
    rz_recv,
):
    sections, xs, zs, micro, rows, model, heads = dims
    width = heads * HDIM
    patches = patch.shape[1]
    section = lax.axis_index("section")
    me = lax.axis_index("dp")
    mx, mz = me // zs, me % zs
    last = sections - 1
    ring = {"x": xs, "z": zs}

    def at(x, z):
        return lax.rem(x + 2 * xs, xs) * zs + lax.rem(z + 2 * zs, zs)

    barrier = pltpu.get_barrier_semaphore()
    for there in (at(mx + 1, mz), at(mx - 1, mz), at(mx, mz + 1), at(mx, mz - 1)):
        pl.semaphore_signal(barrier, inc=1, device_id={"dp": there})

    @pl.when(section > 0)
    def _():
        pl.semaphore_signal(barrier, inc=1, device_id={"section": section - 1})

    @pl.when(section < last)
    def _():
        pl.semaphore_signal(barrier, inc=1, device_id={"section": section + 1})

    target_load = pltpu.make_async_copy(target_hbm, target, load_sem.at[0])
    target_load.start()
    patch_load = pltpu.make_async_copy(patch_hbm, patch, load_sem.at[1])
    patch_load.start()

    half = model // 2
    w = wq_ref[...].astype(jnp.float32)
    o = wo_ref[...].astype(jnp.float32)
    left = jnp.concatenate(
        [
            w[:, :half],
            w[0:8, model : model + half],
            w[16:24, model : model + half],
            w[32:40, model : model + half],
            o[0:16, :half],
        ],
        axis=0,
    )
    right = jnp.concatenate(
        [
            w[:, half:model],
            w[8:16, model : model + half],
            w[24:32, model : model + half],
            jnp.concatenate([o[16:20, :half], o[16:20, half:]], axis=0),
            o[0:16, half:],
        ],
        axis=0,
    )
    slabs[me, :, 0:half] = left.astype(jnp.bfloat16)
    slabs[me, :, half:model] = right.astype(jnp.bfloat16)

    pl.semaphore_wait(barrier, 4 + jnp.minimum(section, 1) + jnp.minimum(last - section, 1))

    def sign(c):
        return 1 - 2 * lax.rem(c + 2 * xs * zs, 2)

    def cut(origin, part):
        if part == 0:
            return slabs.at[origin, pl.ds(0, SPLIT)]
        return slabs.at[origin, pl.ds(SPLIT, slabs.shape[1] - SPLIT)]

    sends = []

    def place(key, receiver):
        part, f, s = key
        if part == 0:
            way1 = sign(mx)
            if receiver:
                oz = mz - f * way1
                way2 = sign(oz)
                return at(mx - s * way2, oz), None
        else:
            way1 = sign(mz)
            if receiver:
                ox = mx - f * way1
                way2 = sign(ox)
                return at(ox, mz - s * way2), None

    def send(key):
        part, f, s = key
        step = 1 if (s > 0 or (s == 0 and f > 0)) else -1
        if part == 0:
            way1 = sign(mx)
            if s == 0:
                origin = at(mx, mz - (f - step) * way1)
                there = at(mx, mz + step * way1)
                sem = send_first.at[part, f + zs]
            else:
                oz = mz - f * way1
                way2 = sign(oz)
                origin = at(mx - (s - step) * way2, oz)
                there = at(mx + step * way2, mz)
                sem = send_second.at[part, f + zs, s + zs]
        else:
            way1 = sign(mz)
            if s == 0:
                origin = at(mx - (f - step) * way1, mz)
                there = at(mx + step * way1, mz)
                sem = send_first.at[part, f + zs]
            else:
                ox = mx - f * way1
                way2 = sign(ox)
                origin = at(ox, mz - (s - step) * way2)
                there = at(mx, mz + step * way2)
                sem = send_second.at[part, f + zs, s + zs]
        copy = pltpu.make_async_remote_copy(
            src_ref=cut(origin, part),
            dst_ref=cut(origin, part),
            send_sem=sem,
            recv_sem=own_recv.at[part, origin],
            device_id={"dp": there},
        )
        copy.start()
        sends.append(copy)

    def after(key):
        part, f, s = key
        first, second = (zs, xs) if part == 0 else (xs, zs)
        flows = {1: first // 2, -1: first - 1 - first // 2}
        cross = {1: second // 2, -1: second - 1 - second // 2}
        if s == 0:
            for way in (1, -1):
                if (f == 0 or (f > 0) == (way > 0)) and abs(f) < flows[way]:
                    send((part, f + way, 0))
            for way in (1, -1):
                send((part, f, way))
        else:
            way = 1 if s > 0 else -1
            if abs(s) < cross[way]:
                send((part, f, s + way))

    plan = gather_plan(xs, zs)
    after((0, 0, 0))
    after((1, 0, 0))

    lane = lax.broadcasted_iota(jnp.int32, (rows, 128), 1)
    sub = lax.broadcasted_iota(jnp.int32, (rows, 128), 0)
    eye = lane == sub
    slot = lax.broadcasted_iota(jnp.int32, (1, rows), 1)
    for m in range(micro):
        keep = keep_ref[m : m + 1, :]
        alive = jnp.where((slot < lengths_ref[m]) & (keep == 1), 1.0, 0.0)
        live_rows[m, :, 0:rows] = jnp.broadcast_to(alive, (8, rows))

    def column(row):
        return jnp.sum(jnp.where(eye[:, :rows], row, 0.0), axis=1, keepdims=True)

    patch_load.wait()

    @pl.when(section == 0)
    def _():
        for m in range(micro):
            chosen = column(visible_ref[m : m + 1, :].astype(jnp.float32))
            spot = lax.broadcasted_iota(jnp.int32, (rows, patches), 1).astype(jnp.float32)
            pick = jnp.where(spot == chosen, 1.0, 0.0).astype(jnp.bfloat16)
            xin[m] = jnp.dot(pick, patch[m], preferred_element_type=jnp.float32).astype(
                jnp.bfloat16
            )
            err_in[m] = jnp.zeros(err_in.shape[1:], jnp.float32)

    for key in plan:
        part = key[0]
        origin, _ = place(key, True)
        pltpu.make_async_remote_copy(
            src_ref=cut(origin, part),
            dst_ref=cut(origin, part),
            send_sem=send_first.at[part, 0],
            recv_sem=own_recv.at[part, origin],
            device_id={"dp": me},
        ).wait_recv()
        after(key)

    @pl.loop(0, xs * zs // 4)
    def _(g):
        r160 = pl.multiple_of(g * 160, 16)
        r80 = pl.multiple_of(g * 80, 16)
        for c in range(0, half, 128):
            a = [slabs[g * 4 + j, :, c : c + 128].astype(jnp.float32) for j in range(4)]
            b = [
                slabs[g * 4 + j, :, half + c : half + c + 128].astype(jnp.float32)
                for j in range(4)
            ]
            qk0 = jnp.concatenate([t[0:40] for t in a], axis=0)
            qk1 = jnp.concatenate([t[0:40] for t in b], axis=0)
            val = []
            o0 = []
            o1 = []
            for t, u in zip(a, b):
                val += [t[40:48], u[40:48], t[48:56], u[48:56], t[56:64]]
                o0 += [t[64:80], u[56:60]]
                o1 += [u[64:80], u[60:64]]
            wqkv[pl.ds(r160, 160), c : c + 128] = qk0.astype(jnp.bfloat16)
            wqkv[pl.ds(r160, 160), half + c : half + c + 128] = qk1.astype(jnp.bfloat16)
            wqkv[pl.ds(r160, 160), model + c : model + c + 128] = jnp.concatenate(
                val, axis=0
            ).astype(jnp.bfloat16)
            wout[pl.ds(r80, 80), c : c + 128] = jnp.concatenate(o0, axis=0).astype(jnp.bfloat16)
            wout[pl.ds(r80, 80), half + c : half + c + 128] = jnp.concatenate(
                o1, axis=0
            ).astype(jnp.bfloat16)

    target_load.wait()
    gain = gain_ref[...].astype(jnp.float32)
    to_next = jnp.minimum(section + 1, last)

    def token_copy(m):
        return pltpu.make_async_remote_copy(
            src_ref=yout.at[m],
            dst_ref=xin.at[m],
            send_sem=x_send.at[m],
            recv_sem=x_recv.at[m],
            device_id={"section": to_next},
        )

    def error_copy(m):
        return pltpu.make_async_remote_copy(
            src_ref=err_out.at[m],
            dst_ref=err_in.at[m],
            send_sem=e_send.at[m],
            recv_sem=e_recv.at[m],
            device_id={"section": to_next},
        )

    def hidden_copy(m):
        return pltpu.make_async_copy(hid.at[m], hidden_hbm.at[m], hid_sem.at[m])

    blocks = width // 128
    feature = lax.broadcasted_iota(jnp.int32, (1, 128), 1)

    @pl.loop(0, micro)
    def _(m):
        @pl.when(section > 0)
        def _():
            token_copy(m).wait_recv()

        alive = live_rows[m, 0:1, 0:rows]
        tokens = xin[m].astype(jnp.float32)
        normed = (normalised(tokens) * gain).astype(jnp.bfloat16)
        step = 640 if (3 * width) % 640 == 0 else 3 * width
        for c in range(0, 3 * width, step):
            qkv[:, c : c + step] = jnp.dot(
                normed, wqkv[:, c : c + step], preferred_element_type=jnp.float32
            ).astype(jnp.bfloat16)

        sums = [None] * blocks
        for h in range(heads):
            low, high = (h * HDIM, (h + 1) * HDIM)
            scores = None
            mine = range(low // 128, (high - 1) // 128 + 1)
            inside = {b: (feature >= low - 128 * b) & (feature < high - 128 * b) for b in mine}
            for b in mine:
                q = qkv[:, 128 * b : 128 * b + 128]
                q = jnp.where(inside[b], q, jnp.zeros_like(q))
                k = qkv[:, width + 128 * b : width + 128 * b + 128]
                term = lax.dot_general(
                    q, k, (((1,), (1,)), ((), ())), preferred_element_type=jnp.float32
                )
                scores = term if scores is None else scores + term
            scores = jnp.where(alive > 0.5, scores * HDIM ** (-0.5), -1e30)
            weights = jnp.exp(scores - jnp.max(scores, -1, keepdims=True))
            prob = (weights / jnp.sum(weights, -1, keepdims=True)).astype(jnp.bfloat16)
            for b in mine:
                v = qkv[:, 2 * width + 128 * b : 2 * width + 128 * b + 128]
                v = jnp.where(inside[b], v, jnp.zeros_like(v))
                term = jnp.dot(prob, v, preferred_element_type=jnp.float32)
                sums[b] = term if sums[b] is None else sums[b] + term
        for b in range(blocks):
            ctx[:, 128 * b : 128 * b + 128] = sums[b].astype(jnp.bfloat16)
        context = ctx[...]
        step = 640 if model % 640 == 0 else model
        for c in range(0, model, step):
            total = jnp.dot(context, wout[:, c : c + step], preferred_element_type=jnp.float32)
            total = total + xin[m, :, c : c + step].astype(jnp.float32)
            yout[m, :, c : c + step] = total.astype(jnp.bfloat16)

        @pl.when(section < last)
        def _():
            token_copy(m).start()

        live_column = column(alive)
        result = yout[m].astype(jnp.float32)
        hid[m] = jnp.where(live_column > 0.5, result, 0.0).astype(jnp.bfloat16)
        hidden_copy(m).start()
        deviation = normalised(result) - target[m].astype(jnp.float32)
        error = jnp.mean(deviation * deviation, -1, keepdims=True)
        error = jnp.where(live_column > 0.5, error, 0.0)
        error = jnp.sum(jnp.where(eye, error, 0.0), axis=0, keepdims=True)

        @pl.when(section > 0)
        def _():
            error_copy(m).wait_recv()

        err_out[m] = err_in[m] + jnp.broadcast_to(error, err_in.shape[1:])

        @pl.when(section < last)
        def _():
            error_copy(m).start()

    def total_copy(there):
        return pltpu.make_async_remote_copy(
            src_ref=tl.at[0],
            dst_ref=tl.at[1],
            send_sem=t_send.at[there],
            recv_sem=t_recv,
            device_id={"section": there},
        )

    @pl.when(section == last)
    def _():
        band = lax.broadcasted_iota(jnp.int32, (8, 128), 0)
        whole = jnp.zeros((8, 128), jnp.float32)
        for m in range(micro):
            whole = jnp.where(band == m, err_out[m], whole)
        tl[0] = whole
        tl[1] = whole
        for there in range(last):
            total_copy(there).start()

    @pl.when(section < last)
    def _():
        total_copy(section).wait_recv()

    band = lax.broadcasted_iota(jnp.int32, (8, 128), 0)
    whole = tl[1]
    token_ref[...] = whole[0:micro, 0:rows]
    own = jnp.broadcast_to(jnp.sum(whole, axis=1, keepdims=True), (8, 128))
    for m in range(micro):
        number = jnp.sum(live_rows[m, :, 0:rows], axis=1, keepdims=True)
        own = jnp.where(band == micro + m, number, own)
    part_own[...] = own
    slots_x[mx] = own

    def x_copy(there, slot):
        return pltpu.make_async_remote_copy(
            src_ref=part_own,
            dst_ref=slots_x.at[slot],
            send_sem=rx_send.at[there],
            recv_sem=rx_recv.at[slot],
            device_id={"dp": there * zs + mz},
        )

    def z_copy(there, slot):
        return pltpu.make_async_remote_copy(
            src_ref=part_mid,
            dst_ref=slots_z.at[slot],
            send_sem=rz_send.at[there],
            recv_sem=rz_recv.at[slot],
            device_id={"dp": mx * zs + there},
        )

    for k in range(1, xs):
        x_copy(lax.rem(mx + k, xs), mx).start()
    for k in range(1, xs):
        there = lax.rem(mx + k, xs)
        x_copy(there, there).wait_recv()
    mid = slots_x[0]
    for k in range(1, xs):
        mid = mid + slots_x[k]
    part_mid[...] = mid
    slots_z[mz] = mid
    for k in range(1, zs):
        z_copy(lax.rem(mz + k, zs), mz).start()
    for k in range(1, zs):
        there = lax.rem(mz + k, zs)
        z_copy(there, there).wait_recv()
    total = slots_z[0]
    for k in range(1, zs):
        total = total + slots_z[k]
    loss_ref[...] = total[0:micro] / total[micro : 2 * micro]

    for copy in sends:
        copy.wait_send()

    @pl.loop(0, micro)
    def _(m):
        hidden_copy(m).wait()

        @pl.when(section < last)
        def _():
            token_copy(m).wait_send()
            error_copy(m).wait_send()

    @pl.when(section == last)
    def _():
        for there in range(last):
            total_copy(there).wait_send()

    for k in range(1, xs):
        x_copy(lax.rem(mx + k, xs), mx).wait_send()
    for k in range(1, zs):
        z_copy(lax.rem(mz + k, zs), mz).wait_send()


def per_device(
    sections, xs, zs, patch_tokens, visible, keep_mask, lengths, qkv_weight, out_weight, norm_gain, targets
):
    micro, _, rows = visible.shape
    patches, model = patch_tokens.shape[2:]
    depth, columns = qkv_weight.shape[1:]
    odepth = out_weight.shape[1]
    heads = columns // (3 * HDIM)
    width = heads * HDIM
    devices = xs * zs
    dims = (sections, xs, zs, micro, rows, model, heads)
    bf, f32 = (jnp.bfloat16, jnp.float32)
    vmem = pl.BlockSpec(memory_space=pltpu.VMEM)
    hbm = pl.BlockSpec(memory_space=pl.ANY)
    dma = pltpu.SemaphoreType.DMA
    hidden, token, loss = pl.pallas_call(
        functools.partial(kernel, dims),
        out_shape=(
            jax.ShapeDtypeStruct((micro, rows, model), bf),
            jax.ShapeDtypeStruct((micro, rows), f32),
            jax.ShapeDtypeStruct((micro, 128), f32),
        ),
        in_specs=[pl.BlockSpec(memory_space=pltpu.SMEM)] + [vmem] * 5 + [hbm] * 2,
        out_specs=(hbm, vmem, vmem),
        scratch_shapes=[
            pltpu.VMEM((devices, depth * 2, model), bf),
            pltpu.VMEM((depth * devices, columns), bf),
            pltpu.VMEM((odepth * devices, model), bf),
            pltpu.VMEM((micro, patches, model), bf),
            pltpu.VMEM((micro, rows, model), bf),
            pltpu.VMEM((micro, rows, model), bf),
            pltpu.VMEM((micro, rows, model), bf),
            pltpu.VMEM((micro, rows, model), bf),
            pltpu.VMEM((rows, columns), bf),
            pltpu.VMEM((rows, width), bf),
            pltpu.VMEM((micro, 8, 128), f32),
            pltpu.VMEM((micro, 8, 128), f32),
            pltpu.VMEM((micro, 8, 128), f32),
            pltpu.VMEM((2, 8, 128), f32),
            pltpu.VMEM((8, 128), f32),
            pltpu.VMEM((8, 128), f32),
            pltpu.VMEM((xs, 8, 128), f32),
            pltpu.VMEM((zs, 8, 128), f32),
            dma((2,)),
            dma((micro,)),
            dma((2, devices)),
            dma((2, 2 * zs)),
            dma((2, 2 * zs, 2 * zs)),
            dma((micro,)),
            dma((micro,)),
            dma((micro,)),
            dma((micro,)),
            dma((sections,)),
            dma,
            dma((xs,)),
            dma((xs,)),
            dma((zs,)),
            dma((zs,)),
        ],
        compiler_params=pltpu.CompilerParams(collective_id=0, has_side_effects=True),
    )(
        lengths,
        visible[:, 0],
        keep_mask[:, 0],
        qkv_weight[0],
        out_weight[0],
        norm_gain,
        patch_tokens[:, 0],
        targets[0, :, 0],
    )
    return (hidden[None, :, None], token[:, None], loss[:, 0])


def solution(mesh):
    sections, devices = (mesh.shape["section"], mesh.shape["dp"])
    placed = (
        P(None, "dp", None, None),
        P(None, "dp", None),
        P(None, "dp", None),
        P(),
        P("section", "dp", None),
        P("section", "dp", None),
        P("section", None),
        P("section", None, "dp", None, None),
    )
    return jax.shard_map(
        functools.partial(per_device, sections, X, devices // X),
        mesh=mesh,
        in_specs=placed,
        out_specs=(P("section", None, "dp", None, None), P(None, "dp", None), P()),
        check_vma=False,
    )
```

time: 576 us -> 181 us (0.31)
  Pallas kernels: 0 us -> 172 us
  starting transfers between devices: 145 us -> 0 us
  waiting for transfers between devices: 127 us -> 0 us
  blocking collectives: 84.5 us -> 0 us
  local copies, waits for them, and re-layouts: 81.9 us -> 7.78 us
  other arithmetic: 51.2 us -> 0 us
  loops' own time: 45.7 us -> 0 us
  matrix products: 22.4 us -> 0 us
  between operations: 14.1 us -> 0.67 us
    pallas_call x0 -> x1, Pallas kernels: none -> 172 us  [per_device(): pl.pallas_call(functools.partial(kernel, dims), out_shape=(jax.ShapeDtype...]
    ppermute x19 -> x0, starting transfers between devices: 140 us -> none  [passed_along(): return lax.ppermute(block, axis, route)]
    all_gather x1 -> x0, waiting for transfers between devices: 97.9 us -> none  [gather_packed(): lines, at, outs = (lax.all_gather(flat, axis), 0, [])]
    all_to_all x1 -> x0, blocking collectives: 84.5 us -> none  [copy_for_each(): lax.all_to_all(jnp.broadcast_to(x[None], (length, *x.shape)), axis, 0, 0,...]
    another operation x20 -> x0, loops' own time: 45.7 us -> none  [the longest x1 37.6 us: per_device(): lax.fori_loop(0, micro_count + sections - 1, advance, start_carry)]
    dynamic_update_slice x38 -> x0, other arithmetic: 35 us -> none  [the longest x19 34.9 us: advance(): lax.dynamic_update_index_in_dim(hidden, jnp.where(active, masked_output,...]
    dynamic_slice x57 -> x0, local copies, waits for them, and re-layouts: 30.5 us -> none  [the longest x19 18.6 us: advance(): hidden[batch_index]]
    ppermute x19 -> x0, waiting for transfers between devices: 23.4 us -> none  [passed_along(): return lax.ppermute(block, axis, route)]
  transfers between devices with their start and end apart: 21 -> 0, of which waited for: 21 -> 0; matrix products, arithmetic and copies ran while one was open for 11% -> 0% of each run, Pallas kernels for 0% -> 0%
where the time goes in v1:
time: 181 us; the launch traced here: 180 us
  Pallas kernels  172 us (95%)
  local copies, waits for them, and re-layouts  7.78 us (4%)
    pallas_call x1, Pallas kernels, per_device(): pl.pallas_call(functools.partial(kernel, dims), out_shape=(jax.ShapeDtype...  172 us
    unnamed x10, local copies, waits for them, and re-layouts  7.15 us

profile of v1, /device:TPU:1, one launch (start us, length us, event | category | flops | bytes accessed | tf_op | source)
XLA Modules:
  0.0 180.3 jit_solution(13036936352486485160)
XLA Ops:
  0.6 0.0 copy-start
  0.6 2.4 %copy.22 = bf16[1,4,1,98,1280]{4,3,1,2,0:T(8,128)(2,1)} copy(bf16[1,4,1,98,1280]{4,1,3,2,0:T(4,128)(2,1)} %param.15) | data formatting | bytes 2007040 | tf_op args[7]
  3.1 0.0 copy-done
  3.1 1.5 copy.21
  4.6 171.9 %shard_map.103 = (bf16[4,98,1280]{2,1,0:T(8,128)(2,1)}, f32[4,98]{1,0:T(4,128)}, f32[4,128]{1,0:T(4,128)}) custom-call(s32[4]{0:T(128)} %lengths_ref.1, s32[4,98]{1,0:T(4,128)} %bitcast.19, s32[4,98]{1,0:T(4,128)} %bitcast.20, bf16[40,1920]{1,0:T(8,128)(2,1)} %bitcast.17, bf16[20,1280]{1,0:T(8,128)(2,1)} %bitcast.18, bf16[1,1280]{1,0:T(2,128)(2,1)} %gain_ref.1, ...), custom_call_target="tpu_custom_call" | custom-call | tf_op jit(solution)/shard_map/pallas_call | solution.py:538
  176.5 0.0 copy-start.1
  176.5 0.0 copy-start.2
  176.5 2.6 %copy.17 = bf16[1,4,1,98,1280]{4,1,3,2,0:T(4,128)(2,1)} copy(bf16[1,4,1,98,1280]{4,3,1,2,0:T(8,128)(2,1)} %bitcast.16) | data formatting | bytes 2007040
  179.1 0.0 copy-done.1
  179.1 0.6 slice_reduce_fusion
  179.7 0.0 copy-done.2
  179.7 0.6 copy.24
Async XLA Ops:
  0.6 2.5 %copy-start = (bf16[4,1,196,1280]{3,0,2,1:T(4,128)(2,1)S(1)}, bf16[4,1,196,1280]{3,0,2,1:T(4,128)(2,1)}, u32[]{:S(2)}) copy-start(bf16[4,1,196,1280]{3,0,2,1:T(4,128)(2,1)} %param.8) | copy-start | bytes 6021124
  176.5 2.6 %copy-start.1 = (f32[4,128]{1,0:T(4,128)S(1)}, f32[4,128]{1,0:T(4,128)}, u32[]{:S(2)}) copy-start(f32[4,128]{1,0:T(4,128)} %get-tuple-element.8) | copy-start | bytes 6148
  176.5 3.2 %copy-start.2 = (f32[4,98]{1,0:T(4,128)S(1)}, f32[4,98]{1,0:T(4,128)}, u32[]{:S(2)}) copy-start(f32[4,98]{1,0:T(4,128)} %get-tuple-element.7) | copy-start | bytes 4708

commit v2 on v1

--- a/solution.py
+++ b/solution.py
@@ -110,8 +110,7 @@
     load_sem,
     hid_sem,
     own_recv,
-    send_first,
-    send_second,
+    slab_send,
     x_send,
     x_recv,
     e_send,
@@ -188,8 +187,6 @@
             return slabs.at[origin, pl.ds(0, SPLIT)]
         return slabs.at[origin, pl.ds(SPLIT, slabs.shape[1] - SPLIT)]
 
-    sends = []
-
     def place(key, receiver):
         part, f, s = key
         if part == 0:
@@ -213,34 +210,29 @@
             if s == 0:
                 origin = at(mx, mz - (f - step) * way1)
                 there = at(mx, mz + step * way1)
-                sem = send_first.at[part, f + zs]
             else:
                 oz = mz - f * way1
                 way2 = sign(oz)
                 origin = at(mx - (s - step) * way2, oz)
                 there = at(mx + step * way2, mz)
-                sem = send_second.at[part, f + zs, s + zs]
         else:
             way1 = sign(mz)
             if s == 0:
                 origin = at(mx - (f - step) * way1, mz)
                 there = at(mx + step * way1, mz)
-                sem = send_first.at[part, f + zs]
             else:
                 ox = mx - f * way1
                 way2 = sign(ox)
                 origin = at(ox, mz - (s - step) * way2)
                 there = at(mx, mz + step * way2)
-                sem = send_second.at[part, f + zs, s + zs]
         copy = pltpu.make_async_remote_copy(
             src_ref=cut(origin, part),
             dst_ref=cut(origin, part),
-            send_sem=sem,
+            send_sem=slab_send,
             recv_sem=own_recv.at[part, origin],
             device_id={"dp": there},
         )
         copy.start()
-        sends.append(copy)
 
     def after(key):
         part, f, s = key
@@ -293,7 +285,7 @@
         pltpu.make_async_remote_copy(
             src_ref=cut(origin, part),
             dst_ref=cut(origin, part),
-            send_sem=send_first.at[part, 0],
+            send_sem=slab_send,
             recv_sem=own_recv.at[part, origin],
             device_id={"dp": me},
         ).wait_recv()
@@ -332,12 +324,13 @@
     gain = gain_ref[...].astype(jnp.float32)
     to_next = jnp.minimum(section + 1, last)
 
-    def token_copy(m):
+    def token_copy(m, i):
+        piece = pl.ds(i * half, half)
         return pltpu.make_async_remote_copy(
-            src_ref=yout.at[m],
-            dst_ref=xin.at[m],
-            send_sem=x_send.at[m],
-            recv_sem=x_recv.at[m],
+            src_ref=yout.at[m, :, piece],
+            dst_ref=xin.at[m, :, piece],
+            send_sem=x_send.at[m, i],
+            recv_sem=x_recv.at[m, i],
             device_id={"section": to_next},
         )
 
@@ -360,7 +353,8 @@
     def _(m):
         @pl.when(section > 0)
         def _():
-            token_copy(m).wait_recv()
+            token_copy(m, 0).wait_recv()
+            token_copy(m, 1).wait_recv()
 
         alive = live_rows[m, 0:1, 0:rows]
         tokens = xin[m].astype(jnp.float32)
@@ -396,15 +390,15 @@
         for b in range(blocks):
             ctx[:, 128 * b : 128 * b + 128] = sums[b].astype(jnp.bfloat16)
         context = ctx[...]
-        step = 640 if model % 640 == 0 else model
-        for c in range(0, model, step):
-            total = jnp.dot(context, wout[:, c : c + step], preferred_element_type=jnp.float32)
-            total = total + xin[m, :, c : c + step].astype(jnp.float32)
-            yout[m, :, c : c + step] = total.astype(jnp.bfloat16)
-
-        @pl.when(section < last)
-        def _():
-            token_copy(m).start()
+        for i in range(2):
+            c = i * half
+            total = jnp.dot(context, wout[:, c : c + half], preferred_element_type=jnp.float32)
+            total = total + xin[m, :, c : c + half].astype(jnp.float32)
+            yout[m, :, c : c + half] = total.astype(jnp.bfloat16)
+
+            @pl.when(section < last)
+            def _():
+                token_copy(m, i).start()
 
         live_column = column(alive)
         result = yout[m].astype(jnp.float32)
@@ -497,8 +491,14 @@
         total = total + slots_z[k]
     loss_ref[...] = total[0:micro] / total[micro : 2 * micro]
 
-    for copy in sends:
-        copy.wait_send()
+    others = slabs.at[pl.ds(0, xs * zs - 1)]
+    pltpu.make_async_remote_copy(
+        src_ref=others,
+        dst_ref=others,
+        send_sem=slab_send,
+        recv_sem=t_recv,
+        device_id={"dp": me},
+    ).wait_send()
 
     @pl.loop(0, micro)
     def _(m):
@@ -506,7 +506,8 @@
 
         @pl.when(section < last)
         def _():
-            token_copy(m).wait_send()
+            token_copy(m, 0).wait_send()
+            token_copy(m, 1).wait_send()
             error_copy(m).wait_send()
 
     @pl.when(section == last)
@@ -566,10 +567,9 @@
             dma((2,)),
             dma((micro,)),
             dma((2, devices)),
-            dma((2, 2 * zs)),
-            dma((2, 2 * zs, 2 * zs)),
-            dma((micro,)),
-            dma((micro,)),
+            dma,
+            dma((micro, 2)),
+            dma((micro, 2)),
             dma((micro,)),
             dma((micro,)),
             dma((sections,)),

time: 181 us -> 176 us (0.972)
  Pallas kernels: 172 us -> 167 us
    pallas_call x1, Pallas kernels: 172 us -> 167 us  [per_device(): pl.pallas_call(functools.partial(kernel, dims), out_shape=(jax.ShapeDtype...]
where the time goes in v2:
time: 176 us; the launch traced here: 175 us
  Pallas kernels  167 us (95%)
  local copies, waits for them, and re-layouts  7.78 us (4%)
    pallas_call x1, Pallas kernels, per_device(): pl.pallas_call(functools.partial(kernel, dims), out_shape=(jax.ShapeDtype...  167 us
    unnamed x10, local copies, waits for them, and re-layouts  7.15 us

profile of v2, /device:TPU:1, one launch (start us, length us, event | category | flops | bytes accessed | tf_op | source)
XLA Modules:
  0.0 175.1 jit_solution(18267350119348285843)
XLA Ops:
  0.6 0.0 copy-start
  0.6 2.4 %copy.22 = bf16[1,4,1,98,1280]{4,3,1,2,0:T(8,128)(2,1)} copy(bf16[1,4,1,98,1280]{4,1,3,2,0:T(4,128)(2,1)} %param.15) | data formatting | bytes 2007040 | tf_op args[7]
  3.1 0.0 copy-done
  3.1 1.5 copy.21
  4.6 166.7 %shard_map.103 = (bf16[4,98,1280]{2,1,0:T(8,128)(2,1)}, f32[4,98]{1,0:T(4,128)}, f32[4,128]{1,0:T(4,128)}) custom-call(s32[4]{0:T(128)} %lengths_ref.1, s32[4,98]{1,0:T(4,128)} %bitcast.19, s32[4,98]{1,0:T(4,128)} %bitcast.20, bf16[40,1920]{1,0:T(8,128)(2,1)} %bitcast.17, bf16[20,1280]{1,0:T(8,128)(2,1)} %bitcast.18, bf16[1,1280]{1,0:T(2,128)(2,1)} %gain_ref.1, ...), custom_call_target="tpu_custom_call" | custom-call | tf_op jit(solution)/shard_map/pallas_call | solution.py:539
  171.3 0.0 copy-start.1
  171.3 0.0 copy-start.2
  171.4 2.6 %copy.17 = bf16[1,4,1,98,1280]{4,1,3,2,0:T(4,128)(2,1)} copy(bf16[1,4,1,98,1280]{4,3,1,2,0:T(8,128)(2,1)} %bitcast.16) | data formatting | bytes 2007040
  173.9 0.0 copy-done.1
  173.9 0.6 slice_reduce_fusion
  174.6 0.0 copy-done.2
  174.6 0.6 copy.24
Async XLA Ops:
  0.6 2.5 %copy-start = (bf16[4,1,196,1280]{3,0,2,1:T(4,128)(2,1)S(1)}, bf16[4,1,196,1280]{3,0,2,1:T(4,128)(2,1)}, u32[]{:S(2)}) copy-start(bf16[4,1,196,1280]{3,0,2,1:T(4,128)(2,1)} %param.8) | copy-start | bytes 6021124
  171.3 2.6 %copy-start.1 = (f32[4,128]{1,0:T(4,128)S(1)}, f32[4,128]{1,0:T(4,128)}, u32[]{:S(2)}) copy-start(f32[4,128]{1,0:T(4,128)} %get-tuple-element.8) | copy-start | bytes 6148
  171.3 3.2 %copy-start.2 = (f32[4,98]{1,0:T(4,128)S(1)}, f32[4,98]{1,0:T(4,128)}, u32[]{:S(2)}) copy-start(f32[4,98]{1,0:T(4,128)} %get-tuple-element.7) | copy-start | bytes 4708
